TPU v7x, 32 devices: a whole 2x2x4 slice. The times are simulated.
32 devices in a mesh: graph: 8 (over y, x, core), rep: 4 (over z).
Axes of the slice: x: 2, y: 2, z: 4, core: 2. Of those that a mesh axis runs over, the one named last changes fastest.
Arguments:
- nodes: bfloat16 [4, 64, 32, 256], P('rep', 'graph'), may hold values from -20 to 20, as said below
- cotangent: bfloat16 [4, 64, 32, 256], P('rep', 'graph'), may hold values from -6 to 6
- live: int32 [4, 64], P('rep', 'graph'), may hold values from 2 to 32, as said below
- partner_first: int32 [4, 64], P('rep', 'graph'), may hold values from 0 to 63, as said below
- partner_size: int32 [4, 64], P('rep', 'graph'), may hold values from 1 to 2
- edge_src: int32 [4, 2048], P('rep', 'graph'), may hold values from 0 to 255, as said below
- edge_dst: int32 [4, 2048], P('rep', 'graph'), may hold values from 0 to 255, as said below
- w_edge1: bfloat16 [512, 512], replicated, may hold values from -0.25 to 0.25
- b_edge: float32 [512], replicated, may hold values from -3 to 3
- w_edge2: bfloat16 [512, 256], replicated, may hold values from -0.25 to 0.25
- w_node1: bfloat16 [768, 512], replicated, may hold values from -0.21875 to 0.21875
- b_node: float32 [512], replicated, may hold values from -3 to 3
- w_node2: bfloat16 [512, 256], replicated, may hold values from -0.25 to 0.25
Outputs:
- updated: bfloat16 [4, 64, 32, 256], P('rep', 'graph')
- d_nodes: bfloat16 [4, 64, 32, 256], P('rep', 'graph')
- g_edge1: float32 [512, 512], P('rep')
- g_bedge: float32 [512], P('rep')
- g_edge2: float32 [512, 256], P('rep')
- g_node1: float32 [768, 512], P('rep')
- g_bnode: float32 [512], P('rep')
- g_node2: float32 [512, 256], P('rep')
Inputs may be any that keep to these rules, and one draw needn't show every extreme that they name: A graph is one or two consecutive granules of one device, and every granule of a graph but its last is full; rows beyond live are padding. `partner_first`: index within the replica of the first granule of the partner graph, the same for all granules of a graph; pairing is mutual. Graphs in the lower half of a device's 8 granules pair with graphs in the upper half of some device's granules; the upper-half graphs of one device have partners on distinct devices. Within a replica every half of every device holds the same number of two-granule graphs. `edge_src`: row index within the device (granule times 32 plus row); both ends of an edge are live rows of the same graph. `edge_dst`: as edge_src. `nodes`: padding rows are zero.
All inputs are finite; a program needn't handle non-finite values.
Results may differ from a plain program's by a relative error of at most 0.023.
Values may be sent and summed in bfloat16 or wider, within the bound.
A program may use at most 128 MiB of HBM per device.

v0:
```python
import jax
import jax.numpy as jnp
from jax import lax
from jax.sharding import PartitionSpec as P

GMAX = 2


def silu_slope(values):
    sigmoid_value = jax.nn.sigmoid(values)
    return sigmoid_value * (1.0 + values * (1.0 - sigmoid_value))


def attend(queries, key_rows, key_mask):
    scale_factor = queries.shape[-1] ** (-0.5)
    scores = (
        jnp.einsum("gqh,gkh->gqk", queries, key_rows, preferred_element_type=jnp.float32)
        * scale_factor
    )
    scores = jnp.where(key_mask[:, None, :], scores, -jnp.inf)
    highest = jnp.max(scores, axis=-1, keepdims=True)
    powers = jnp.exp(scores - highest)
    softmax_out = powers / jnp.sum(powers, axis=-1, keepdims=True)
    softmax_low = softmax_out.astype(jnp.bfloat16)
    context = jnp.einsum("gqk,gkh->gqh", softmax_low, key_rows, preferred_element_type=jnp.float32)
    moved_rows = (queries.astype(jnp.float32) - context).astype(jnp.bfloat16)
    return (moved_rows, softmax_out, softmax_low)


def attend_back(queries, key_rows, softmax_out, softmax_low, grad_moved):
    scale_factor = queries.shape[-1] ** (-0.5)
    negated = -grad_moved
    grad_probs = jnp.einsum("gqh,gkh->gqk", negated, key_rows, preferred_element_type=jnp.float32)
    grad_keys = jnp.einsum("gqk,gqh->gkh", softmax_low, negated, preferred_element_type=jnp.float32)
    inner_sum = jnp.sum(softmax_out * grad_probs, axis=-1, keepdims=True)
    grad_scores = (softmax_out * (grad_probs - inner_sum) * scale_factor).astype(jnp.bfloat16)
    grad_queries = jnp.einsum(
        "gqk,gkh->gqh", grad_scores, key_rows, preferred_element_type=jnp.float32
    ) + grad_moved.astype(jnp.float32)
    grad_keys = grad_keys + jnp.einsum(
        "gqk,gqh->gkh", grad_scores, queries, preferred_element_type=jnp.float32
    )
    return (grad_queries, grad_keys)


def message_forward(node_rows, w_edge1, b_edge, w_edge2, sources, targets):
    state_width = node_rows.shape[1]
    pre_target = (
        jnp.dot(node_rows, w_edge1[:state_width], preferred_element_type=jnp.float32) + b_edge
    ).astype(jnp.bfloat16)
    pre_source = jnp.dot(
        node_rows, w_edge1[state_width:], preferred_element_type=jnp.float32
    ).astype(jnp.bfloat16)
    summed = pre_target[targets].astype(jnp.float32) + pre_source[sources].astype(jnp.float32)
    gathered = jax.ops.segment_sum(
        jax.nn.silu(summed), targets, num_segments=node_rows.shape[0]
    ).astype(jnp.bfloat16)
    message = jnp.dot(gathered, w_edge2, preferred_element_type=jnp.float32).astype(jnp.bfloat16)
    return (message, gathered, summed)


def message_backward(node_rows, w_edge1, w_edge2, sources, targets, gathered, summed, grad_message):
    state_width = node_rows.shape[1]
    grad_w2 = jnp.einsum("rf,rh->fh", gathered, grad_message, preferred_element_type=jnp.float32)
    grad_gathered = jnp.einsum(
        "rh,fh->rf", grad_message, w_edge2, preferred_element_type=jnp.float32
    ).astype(jnp.bfloat16)
    edge_grad = grad_gathered[targets].astype(jnp.float32) * silu_slope(summed)
    grad_target = jax.ops.segment_sum(edge_grad, targets, num_segments=node_rows.shape[0]).astype(
        jnp.bfloat16
    )
    grad_source = jax.ops.segment_sum(edge_grad, sources, num_segments=node_rows.shape[0]).astype(
        jnp.bfloat16
    )
    grad_w1 = jnp.concatenate(
        [
            jnp.einsum("rh,rf->hf", node_rows, grad_target, preferred_element_type=jnp.float32),
            jnp.einsum("rh,rf->hf", node_rows, grad_source, preferred_element_type=jnp.float32),
        ],
        axis=0,
    )
    grad_bias = jnp.sum(grad_target.astype(jnp.float32), axis=0)
    grad_rows = jnp.einsum(
        "rf,hf->rh", grad_target, w_edge1[:state_width], preferred_element_type=jnp.float32
    ) + jnp.einsum(
        "rf,hf->rh", grad_source, w_edge1[state_width:], preferred_element_type=jnp.float32
    )
    return (grad_rows, grad_w1, grad_bias, grad_w2)


def update_forward(node_rows, message, moved_flat, w_node1, b_node, w_node2, row_mask):
    state_width = node_rows.shape[1]
    hidden_pre = (
        jnp.dot(node_rows, w_node1[:state_width], preferred_element_type=jnp.float32)
        + jnp.dot(
            message, w_node1[state_width : 2 * state_width], preferred_element_type=jnp.float32
        )
        + jnp.dot(moved_flat, w_node1[2 * state_width :], preferred_element_type=jnp.float32)
        + b_node
    )
    active = jax.nn.silu(hidden_pre).astype(jnp.bfloat16)
    updated = jnp.where(
        row_mask,
        node_rows.astype(jnp.float32)
        + jnp.dot(active, w_node2, preferred_element_type=jnp.float32),
        0.0,
    ).astype(jnp.bfloat16)
    return (updated, hidden_pre, active)


def update_backward(node_rows, message, moved_flat, w_node1, w_node2, hidden_pre, active, grad_out):
    state_width = node_rows.shape[1]
    grad_w2 = jnp.einsum("rf,rh->fh", active, grad_out, preferred_element_type=jnp.float32)
    grad_hidden = (
        jnp.einsum("rh,fh->rf", grad_out, w_node2, preferred_element_type=jnp.float32)
        * silu_slope(hidden_pre)
    ).astype(jnp.bfloat16)
    grad_w1 = jnp.concatenate(
        [
            jnp.einsum("rh,rf->hf", node_rows, grad_hidden, preferred_element_type=jnp.float32),
            jnp.einsum("rh,rf->hf", message, grad_hidden, preferred_element_type=jnp.float32),
            jnp.einsum("rh,rf->hf", moved_flat, grad_hidden, preferred_element_type=jnp.float32),
        ],
        axis=0,
    )
    grad_bias = jnp.sum(grad_hidden.astype(jnp.float32), axis=0)
    grad_rows = grad_out.astype(jnp.float32) + jnp.einsum(
        "rf,hf->rh", grad_hidden, w_node1[:state_width], preferred_element_type=jnp.float32
    )
    grad_message = jnp.einsum(
        "rf,hf->rh",
        grad_hidden,
        w_node1[state_width : 2 * state_width],
        preferred_element_type=jnp.float32,
    ).astype(jnp.bfloat16)
    grad_moved = jnp.einsum(
        "rf,hf->rh", grad_hidden, w_node1[2 * state_width :], preferred_element_type=jnp.float32
    ).astype(jnp.bfloat16)
    return (grad_rows, grad_message, grad_moved, grad_w1, grad_bias, grad_w2)


def on_device(
    nodes,
    cotangent,
    live,
    partner_first,
    partner_size,
    edge_src,
    edge_dst,
    w_edge1,
    b_edge,
    w_edge2,
    w_node1,
    b_node,
    w_node2,
):
    local_nodes = nodes[0]
    granules, block_rows, state_width = local_nodes.shape
    half_count = granules // 2
    peer_count = lax.axis_size("graph")
    live_counts = live[0]
    partners = partner_first[0]
    partner_device = partners // granules
    same_before = jnp.concatenate([jnp.zeros((1,), jnp.bool_), partners[1:] == partners[:-1]])
    place_index = same_before.astype(jnp.int32)
    positions = jnp.arange(block_rows, dtype=jnp.int32)
    spans = jnp.arange(GMAX, dtype=jnp.int32)
    row_mask = (positions[None, :] < live_counts[:, None]).reshape(-1, 1)
    node_rows = local_nodes.reshape(-1, state_width)
    sources = edge_src[0]
    targets = edge_dst[0]
    slot_count = peer_count * 2 * GMAX
    send_offset = jnp.where(jnp.arange(granules, dtype=jnp.int32) < half_count, GMAX, 0)
    send_slot = partner_device * (2 * GMAX) + send_offset + place_index
    outgoing = (
        jnp.zeros((slot_count, block_rows, state_width), jnp.bfloat16)
        .at[send_slot]
        .set(local_nodes)
    )
    lives_out = jnp.zeros((slot_count,), jnp.int32).at[send_slot].set(live_counts)
    arrived, arrived_lives = (
        lax.all_to_all(outgoing, "graph", split_axis=0, concat_axis=0, tiled=True),
        lax.all_to_all(lives_out, "graph", split_axis=0, concat_axis=0, tiled=True),
    )
    message, gathered, summed = message_forward(
        node_rows, w_edge1, b_edge, w_edge2, sources, targets
    )
    read_slot = (
        partner_device[:, None] * (2 * GMAX) + (GMAX - send_offset)[:, None] + spans[None, :]
    )
    keys_all = arrived[read_slot].reshape(granules, GMAX * block_rows, state_width)
    mask_all = (positions[None, None, :] < arrived_lives[read_slot][:, :, None]).reshape(
        granules, GMAX * block_rows
    )
    moved_rows, probs_all, low_all = attend(local_nodes, keys_all, mask_all)
    moved_flat = moved_rows.reshape(-1, state_width)
    updated, hidden_pre, active = update_forward(
        node_rows, message, moved_flat, w_node1, b_node, w_node2, row_mask
    )
    grad_out = jnp.where(
        row_mask, cotangent[0].reshape(-1, state_width), jnp.zeros((), jnp.bfloat16)
    )
    grad_rows, grad_message, grad_moved, grad_n1, grad_bn, grad_n2 = update_backward(
        node_rows, message, moved_flat, w_node1, w_node2, hidden_pre, active, grad_out
    )
    grad_moved_blocks = grad_moved.reshape(granules, block_rows, state_width)
    query_all, key_all = attend_back(local_nodes, keys_all, probs_all, low_all, grad_moved_blocks)
    slot_grad = (
        jnp.zeros((slot_count, block_rows, state_width), jnp.float32)
        .at[read_slot.reshape(-1)]
        .add(key_all.reshape(granules * GMAX, block_rows, state_width))
    )
    back_grad = lax.all_to_all(
        slot_grad.astype(jnp.bfloat16), "graph", split_axis=0, concat_axis=0, tiled=True
    ).astype(slot_grad.dtype)
    attention_grad = query_all + back_grad[send_slot]
    message_rows, grad_e1, grad_be, grad_e2 = message_backward(
        node_rows, w_edge1, w_edge2, sources, targets, gathered, summed, grad_message
    )
    total_grad = grad_rows + attention_grad.reshape(-1, state_width) + message_rows
    d_nodes = jnp.where(row_mask, total_grad, 0.0).astype(jnp.bfloat16)
    partial_grads = (grad_e1, grad_be, grad_e2, grad_n1, grad_bn, grad_n2)
    summed_all = lax.psum(
        (
            partial_grads[0],
            partial_grads[1],
            partial_grads[2],
            partial_grads[3],
            partial_grads[4],
            partial_grads[5],
        ),
        ("graph", "rep"),
    )
    replica_index = lax.axis_index("rep")
    replica_count = lax.axis_size("rep")
    shares = tuple(
        (
            lax.dynamic_slice_in_dim(
                summed_grad,
                replica_index * (summed_grad.shape[0] // replica_count),
                summed_grad.shape[0] // replica_count,
                0,
            )
            for summed_grad in summed_all
        )
    )
    scale_factor = (lax.axis_size("graph") * lax.axis_size("rep") * granules * block_rows) ** (-0.5)
    scaled = tuple((summed_grad * scale_factor for summed_grad in shares))
    return (
        updated.reshape(1, granules, block_rows, state_width),
        d_nodes.reshape(1, granules, block_rows, state_width),
        scaled[0],
        scaled[1],
        scaled[2],
        scaled[3],
        scaled[4],
        scaled[5],
    )


def solution(mesh):
    placed = (
        P("rep", "graph", None, None),
        P("rep", "graph", None, None),
        P("rep", "graph"),
        P("rep", "graph"),
        P("rep", "graph"),
        P("rep", "graph"),
        P("rep", "graph"),
        P(),
        P(),
        P(),
        P(),
        P(),
        P(),
    )
    return jax.shard_map(
        on_device,
        mesh=mesh,
        in_specs=placed,
        out_specs=(
            P("rep", "graph", None, None),
            P("rep", "graph", None, None),
            P("rep", None),
            P("rep"),
            P("rep", None),
            P("rep", None),
            P("rep"),
            P("rep", None),
        ),
        check_vma=False,
    )
```

profile of v0, /device:TPU:0, one launch (start us, length us, event | category | flops | bytes accessed | tf_op | source)
XLA Modules:
  0.0 223.0 jit_solution(15581898955150633358)
XLA Ops:
  7.2 0.8 compare_bitcast_fusion
  8.1 0.7 fusion.59
  8.8 0.7 scatter_custom_fusion.1
  9.5 0.7 all_to_all.14
  10.2 5.2 %all-to-all-start = ((s32[8,4,1]{1,2,0:T(1,128)}), s32[8,4,1]{1,2,0:T(1,128)S(1)}, u32[]{:S(2)}, u32[]{:S(2)}) async-start(s32[8,4,1]{1,2,0:T(1,128)} %bitcast.11), calls=%async_computation | async-start | bytes 8192 | tf_op jit(solution)/shard_map/all_to_all | solution.py:183
  15.4 0.7 iota_compare_fusion
  17.0 1.2 fusion.43
  18.2 1.2 convolution_convert_fusion.1
  20.5 1.2 gather_fusion.1
  21.6 1.2 gather_fusion
  22.8 2.4 %scatter_custom_fusion = f32[256,512]{1,0:T(8,128)S(1)} fusion(s32[256]{0:T(256)S(1)} %bitcast.123, bf16[256,512]{1,0:T(8,128)(2,1)S(1)} %gather_fusion.1, bf16[256,512]{1,0:T(8,128)(2,1)S(1)} %gather_fusion, f32[]{:T(128)} %constant.24.clone.1, f32[]{:T(128)} %constant.21.clone.1), kind=kCustom, calls=%fused_computation.59 | custom fusion | flops 1048576 | bytes 1048584 | tf_op jit(solution)/shard_map/scatter-add | solution.py:55
  25.4 1.0 convolution_add_fusion.2
  26.5 0.9 broadcast_in_dim.80
  27.3 2.1 scatter_fusion
  29.4 4.2 %all-to-all-start.1 = ((bf16[32,32,256]{2,1,0:T(8,128)(2,1)}), bf16[32,32,256]{2,1,0:T(8,128)(2,1)}, u32[]{:S(2)}, u32[]{:S(2)}) async-start(bf16[32,32,256]{2,1,0:T(8,128)(2,1)} %scatter_fusion), calls=%async_computation.1 | async-start | bytes 1048576 | tf_op jit(solution)/shard_map/all_to_all | solution.py:182
  36.2 7.2 %all-to-all-done.1 = bf16[32,32,256]{2,1,0:T(8,128)(2,1)} async-done(((bf16[32,32,256]{2,1,0:T(8,128)(2,1)}), bf16[32,32,256]{2,1,0:T(8,128)(2,1)}, u32[]{:S(2)}, u32[]{:S(2)}) %all-to-all-start.1) | async-done | bytes 524320 | tf_op jit(solution)/shard_map/all_to_all | solution.py:182
  43.4 1.6 gather_fusion.3
  45.2 0.8 fusion.72
  48.3 0.9 fusion.73
  49.2 1.7 fusion.52
  50.9 0.9 fusion.74
  52.0 1.2 convolution_convert_fusion
  53.2 1.1 fusion.47
  54.3 1.1 fusion.76
  55.3 1.0 fusion.75
  56.4 1.1 convolution_bitcast_fusion
  57.5 1.2 fusion.71
  58.7 1.2 gather_fusion.5
  59.8 2.6 %scatter_custom_fusion.4 = f32[256,512]{1,0:T(8,128)S(1)} fusion(s32[256]{0:T(256)} %bitcast.122, f32[]{:T(128)} %constant.21.clone.1, bf16[256,512]{1,0:T(8,128)(2,1)S(1)} %gather_fusion.5, bf16[256,512]{1,0:T(8,128)(2,1)S(1)} %gather_fusion.1, bf16[256,512]{1,0:T(8,128)(2,1)S(1)} %gather_fusion), kind=kCustom, calls=%fused_computation.68 | custom fusion | flops 1703936 | bytes 1311232 | tf_op jit(solution)/shard_map/scatter-add | solution.py:69
  62.4 2.8 %scatter_custom_fusion.5 = f32[256,512]{1,0:T(8,128)S(1)} fusion(s32[256]{0:T(256)} %bitcast.124, f32[]{:T(128)} %constant.21.clone.1, bf16[256,512]{1,0:T(8,128)(2,1)S(1)} %gather_fusion.5, bf16[256,512]{1,0:T(8,128)(2,1)S(1)} %gather_fusion.1, bf16[256,512]{1,0:T(8,128)(2,1)S(1)} %gather_fusion), kind=kCustom, calls=%fused_computation.66 | custom fusion | flops 1703936 | bytes 1311232 | tf_op jit(solution)/shard_map/scatter-add | solution.py:72
  65.7 1.1 pad_maximum_fusion.1
  67.0 1.3 pad_maximum_fusion
  68.4 2.3 %convolution_add_fusion = f32[8,64,256]{2,1,0:T(8,128)S(1)} fusion(f32[8,64,256]{2,1,0:T(8,128)S(1)} %fusion.52, f32[8,32,64]{2,1,0:T(8,128)} %fusion.74, bf16[1,8,32,256]{3,2,1,0:T(8,128)(2,1)S(1)} %copy-done.1, f32[8,32,64]{2,1,0:T(8,128)} %get-tuple-element.15, f32[8,32]{1,0:T(8,128)S(1)} %get-tuple-element.14), kind=kOutput, calls=%fused_computation.18 | convolution fusion | flops 8634687 | bytes 1311744 | tf_op jit(solution)/shard_map/gqk,gqh->gkh/dot_general | solution.py:40
  70.8 1.3 scatter_fusion.1
  72.2 0.9 convert_element_type.113
  73.1 3.6 %all-to-all-start.2 = ((bf16[32,32,256]{2,1,0:T(8,128)(2,1)}), bf16[32,32,256]{2,1,0:T(8,128)(2,1)S(1)}, u32[]{:S(2)}, u32[]{:S(2)}) async-start(bf16[32,32,256]{2,1,0:T(8,128)(2,1)} %convert_element_type.113), calls=%async_computation.2 | async-start | bytes 1048576 | tf_op jit(solution)/shard_map/all_to_all | solution.py:213
  76.7 46.2 %all-reduce = (f32[512]{0:T(512)S(1)}, f32[512]{0:T(512)S(1)}) all-reduce(f32[512]{0:T(512)S(1)} %convert_reduce_fusion.1, f32[512]{0:T(512)S(1)} %get-tuple-element.18), channel_id=1, replica_groups=mesh['graph'=8,'rep'=4] {'graph','rep'}, use_global_device_ids=true, to_apply=%region_11.12 | all-reduce | flops 1024 | bytes 8192 | tf_op jit(solution)/shard_map/psum | solution.py:223
  124.4 2.0 fusion.11
  126.4 1.1 convert_element_type.114
  127.6 1.8 gather_fusion.4
  129.4 2.2 fusion.6
  131.5 1.2 fusion.7
  132.8 0.9 fusion.13
  133.7 75.8 %all-reduce.4.cloned.1.call-done = (f32[512,512]{1,0:T(8,128)}, f32[512,256]{1,0:T(8,128)}, f32[768,512]{1,0:T(8,128)}, f32[512,256]{1,0:T(8,128)}) async-done(((f32[512,512]{1,0:T(8,128)}, f32[512,256]{1,0:T(8,128)}, f32[768,512]{1,0:T(8,128)}, f32[512,256]{1,0:T(8,128)}), (f32[512,512]{1,0:T(8,128)}, f32[512,256]{1,0:T(8,128)}, f32[768,512]{1,0:T(8,128)}, ...) | async-done | bytes 3670032 | tf_op jit(solution)/shard_map/psum | solution.py:223
  209.5 1.7 dynamic-slice_multiply_fusion.1
  211.2 1.6 dynamic-slice_multiply_fusion.3
  212.8 1.6 dynamic-slice_multiply_fusion.2
  214.3 1.8 dynamic-slice_multiply_fusion
  (95 shorter events, 9.6 us)
Async XLA Ops:
  7.2 40.3 %copy-start = (bf16[512,256]{1,0:T(8,128)(2,1)S(1)}, bf16[512,256]{1,0:T(8,128)(2,1)}, u32[]{:S(2)}) copy-start(bf16[512,256]{1,0:T(8,128)(2,1)} %param.24) | copy-start | bytes 786436
  7.2 12.3 %copy-start.1 = (bf16[1,8,32,256]{3,2,1,0:T(8,128)(2,1)S(1)}, bf16[1,8,32,256]{3,2,1,0:T(8,128)(2,1)}, u32[]{:S(2)}) copy-start(bf16[1,8,32,256]{3,2,1,0:T(8,128)(2,1)} %param.13) | copy-start | bytes 393220
  7.2 12.3 %copy-start.6 = (bf16[512,512]{1,0:T(8,128)(2,1)S(1)}, bf16[512,512]{1,0:T(8,128)(2,1)}, u32[]{:S(2)}) copy-start(bf16[512,512]{1,0:T(8,128)(2,1)} %param.19) | copy-start | bytes 1572868
  7.2 12.2 %copy-start.24 = (s32[1,256]{1,0:T(1,128)S(1)}, s32[1,256]{1,0:T(1,128)}, u32[]{:S(2)}) copy-start(s32[1,256]{1,0:T(1,128)} %param.18) | copy-start | bytes 3076
  7.2 12.2 %copy-start.25 = (s32[1,256]{1,0:T(1,128)S(1)}, s32[1,256]{1,0:T(1,128)}, u32[]{:S(2)}) copy-start(s32[1,256]{1,0:T(1,128)} %param.17) | copy-start | bytes 3076
  7.2 12.3 %copy-start.20 = (f32[512]{0:T(512)S(1)}, f32[512]{0:T(512)}, u32[]{:S(2)}) copy-start(f32[512]{0:T(512)} %param.20) | copy-start | bytes 6148
  10.2 19.2 %all-to-all-start = ((s32[8,4,1]{1,2,0:T(1,128)}), s32[8,4,1]{1,2,0:T(1,128)S(1)}, u32[]{:S(2)}, u32[]{:S(2)}) async-start(s32[8,4,1]{1,2,0:T(1,128)} %bitcast.11), calls=%async_computation | async-start | bytes 8192 | tf_op jit(solution)/shard_map/all_to_all | solution.py:183
  21.6 3.6 %copy-start.9 = (bf16[512,256]{1,0:T(8,128)(2,1)S(1)}, bf16[512,256]{1,0:T(8,128)(2,1)}, u32[]{:S(2)}) copy-start(bf16[512,256]{1,0:T(8,128)(2,1)} %param.21) | copy-start | bytes 786436
  22.8 2.6 %copy-start.2 = (bf16[768,512]{1,0:T(8,128)(2,1)S(1)}, bf16[768,512]{1,0:T(8,128)(2,1)}, u32[]{:S(2)}) copy-start(bf16[768,512]{1,0:T(8,128)(2,1)} %param.22) | copy-start | bytes 2359300
  25.4 8.4 %copy-start.18 = (bf16[1,8,32,256]{3,2,1,0:T(8,128)(2,1)S(1)}, bf16[1,8,32,256]{3,2,1,0:T(8,128)(2,1)}, u32[]{:S(2)}) copy-start(bf16[1,8,32,256]{3,2,1,0:T(8,128)(2,1)} %param.14) | copy-start | bytes 393220
  29.4 14.0 %all-to-all-start.1 = ((bf16[32,32,256]{2,1,0:T(8,128)(2,1)}), bf16[32,32,256]{2,1,0:T(8,128)(2,1)}, u32[]{:S(2)}, u32[]{:S(2)}) async-start(bf16[32,32,256]{2,1,0:T(8,128)(2,1)} %scatter_fusion), calls=%async_computation.1 | async-start | bytes 1048576 | tf_op jit(solution)/shard_map/all_to_all | solution.py:182
  33.6 175.9 %all-reduce.4.cloned.1.call-start = ((), (), s32[]{:S(2)}) async-start(), calls=%async_computation.3 | async-start | bytes 7340032 | tf_op jit(solution)/shard_map/psum | solution.py:223
  33.7 2.2 copy-start.22
  34.0 13.5 %copy-start.11 = (bf16[256,256]{1,0:T(8,128)(2,1)}, bf16[256,256]{1,0:T(8,128)(2,1)S(1)}, u32[]{:S(2)}) copy-start(bf16[256,256]{1,0:T(8,128)(2,1)S(1)} %bitcast_select_fusion) | copy-start | bytes 393220
  35.9 11.3 %copy-start.8 = (f32[256,512]{1,0:T(8,128)S(1)}, f32[256,512]{1,0:T(8,128)}, u32[]{:S(2)}) copy-start(f32[256,512]{1,0:T(8,128)} %convolution_add_fusion.2) | copy-start | bytes 1572868
  35.9 11.3 %copy-start.21 = (f32[512]{0:T(512)S(1)}, f32[512]{0:T(512)}, u32[]{:S(2)}) copy-start(f32[512]{0:T(512)} %param.23) | copy-start | bytes 6148
  45.2 1.3 copy-start.10
  46.5 0.7 copy-start.16
  47.5 0.8 copy-start.14
  50.8 3.4 %copy-start.17 = (bf16[8,32,256]{2,1,0:T(8,128)(2,1)S(1)}, bf16[8,32,256]{2,1,0:T(8,128)(2,1)}, u32[]{:S(2)}) copy-start(bf16[8,32,256]{2,1,0:T(8,128)(2,1)} %copy-done.16) | copy-start | bytes 393220
  54.3 3.2 %copy-start.12 = (bf16[256,256]{1,0:T(8,128)(2,1)S(1)}, bf16[256,256]{1,0:T(8,128)(2,1)}, u32[]{:S(2)}) copy-start(bf16[256,256]{1,0:T(8,128)(2,1)} %copy-done.11) | copy-start | bytes 393220
  54.3 3.2 %copy-start.15 = (f32[256,512]{1,0:T(8,128)S(1)}, f32[256,512]{1,0:T(8,128)}, u32[]{:S(2)}) copy-start(f32[256,512]{1,0:T(8,128)} %copy-done.14) | copy-start | bytes 1572868
  65.4 1.4 copy-start.3
  65.4 1.3 copy-start.4
  65.4 1.6 copy-start.5
  68.3 2.5 %copy-start.26 = (s32[16]{0:T(128)S(1)}, s32[16]{0:T(128)}, u32[]{:S(2)}) copy-start(s32[16]{0:T(128)} %fusion.60) | copy-start | bytes 196
  73.1 51.1 %copy-start.7 = (bf16[512,512]{1,0:T(8,128)(2,1)S(1)}, bf16[512,512]{1,0:T(8,128)(2,1)}, u32[]{:S(2)}) copy-start(bf16[512,512]{1,0:T(8,128)(2,1)} %param.19) | copy-start | bytes 1572868
  73.1 51.3 %copy-start.23 = (pred[256]{0:T(512)(128)(4,1)S(1)}, pred[256]{0:T(512)(128)(4,1)}, u32[]{:S(2)}) copy-start(pred[256]{0:T(512)(128)(4,1)} %copy-done.22) | copy-start | bytes 772
  73.1 53.4 %all-to-all-start.2 = ((bf16[32,32,256]{2,1,0:T(8,128)(2,1)}), bf16[32,32,256]{2,1,0:T(8,128)(2,1)S(1)}, u32[]{:S(2)}, u32[]{:S(2)}) async-start(bf16[32,32,256]{2,1,0:T(8,128)(2,1)} %convert_element_type.113), calls=%async_computation.2 | async-start | bytes 1048576 | tf_op jit(solution)/shard_map/all_to_all | solution.py:213
  126.4 2.9 %copy-start.19 = (bf16[256,256]{1,0:T(8,128)(2,1)S(1)}, bf16[256,256]{1,0:T(8,128)(2,1)}, u32[]{:S(2)}) copy-start(bf16[256,256]{1,0:T(8,128)(2,1)} %get-tuple-element.17) | copy-start | bytes 393220
  126.4 5.1 %copy-start.13 = (bf16[256,256]{1,0:T(8,128)(2,1)S(1)}, bf16[256,256]{1,0:T(8,128)(2,1)}, u32[]{:S(2)}) copy-start(bf16[256,256]{1,0:T(8,128)(2,1)} %copy-done.11) | copy-start | bytes 393220
Sparse Core Ops, SparseCore 0:
  68.5 141.0 all-reduce.3
where the time goes:
time: 224 us; the launch traced here: 223 us
  waiting for transfers between devices  83.1 us (37%)
  blocking collectives  46.2 us (21%)
  other arithmetic  26.5 us (12%)
  matrix products  25 us (11%)
  local copies, waits for them, and re-layouts  14.6 us (7%)
  between operations  14.6 us (7%)
  starting transfers between devices  13 us (6%)
    psum x1, waiting for transfers between devices, on_device(): lax.psum((partial_grads[0], partial_grads[1], partial_grads[2], partial_g...  75.8 us
    psum x1, blocking collectives, on_device(): lax.psum((partial_grads[0], partial_grads[1], partial_grads[2], partial_g...  46.2 us
    mul x6, other arithmetic, on_device(): scaled = tuple((summed_grad * scale_factor for summed_grad in shares))  7.76 us
    all_to_all x1, waiting for transfers between devices, on_device(): lax.all_to_all(outgoing, 'graph', split_axis=0, concat_axis=0, tiled=True)  7.23 us
    all_to_all x1, starting transfers between devices, on_device(): lax.all_to_all(lives_out, 'graph', split_axis=0, concat_axis=0, tiled=True)  5.2 us
  transfers between devices with their start and end apart: 4, of which 2 were waited for; matrix products, arithmetic and copies ran while one was open for 14% of the time, Pallas kernels for 0%

commit v1 on v0

--- a/solution.py
+++ b/solution.py
@@ -220,7 +220,7 @@
     total_grad = grad_rows + attention_grad.reshape(-1, state_width) + message_rows
     d_nodes = jnp.where(row_mask, total_grad, 0.0).astype(jnp.bfloat16)
     partial_grads = (grad_e1, grad_be, grad_e2, grad_n1, grad_bn, grad_n2)
-    summed_all = lax.psum(
+    half = lax.psum(
         (
             partial_grads[0],
             partial_grads[1],
@@ -229,8 +229,9 @@
             partial_grads[4],
             partial_grads[5],
         ),
-        ("graph", "rep"),
-    )
+        "rep",
+    )
+    summed_all = lax.psum(half, "graph")
     replica_index = lax.axis_index("rep")
     replica_count = lax.axis_size("rep")
     shares = tuple(

time: 224 us -> 298 us (1.33)
  waiting for transfers between devices: 83.1 us -> 182 us
  blocking collectives: 46.2 us -> 22.8 us
    psum x1, waiting for transfers between devices: 75.8 us -> 134 us  [on_device(): lax.psum((partial_grads[0], partial_grads[1], partial_grads[2], partial_g...]
    psum x0 -> x1, waiting for transfers between devices: none -> 41.2 us  [on_device(): summed_all = lax.psum(half, 'graph')]
    psum x1, blocking collectives: 46.2 us -> 9.67 us  [on_device(): lax.psum((partial_grads[0], partial_grads[1], partial_grads[2], partial_g...]
    psum x0 -> x1, blocking collectives: none -> 13.1 us  [on_device(): summed_all = lax.psum(half, 'graph')]
  transfers between devices with their start and end apart: 4 -> 5, of which waited for: 2 -> 3; matrix products, arithmetic and copies ran while one was open for 14% -> 12% of each run, Pallas kernels for 0% -> 0%
where the time goes in v1:
time: 298 us; the launch traced here: 297 us
  waiting for transfers between devices  182 us (61%)
  other arithmetic  27 us (9%)
  matrix products  23.3 us (8%)
  blocking collectives  22.8 us (8%)
  between operations  14.6 us (5%)
  local copies, waits for them, and re-layouts  14.4 us (5%)
  starting transfers between devices  13.3 us (4%)
    psum x1, waiting for transfers between devices, on_device(): lax.psum((partial_grads[0], partial_grads[1], partial_grads[2], partial_g...  134 us
    psum x1, waiting for transfers between devices, on_device(): summed_all = lax.psum(half, 'graph')  41.2 us
    psum x1, blocking collectives, on_device(): summed_all = lax.psum(half, 'graph')  13.1 us
    psum x1, blocking collectives, on_device(): lax.psum((partial_grads[0], partial_grads[1], partial_grads[2], partial_g...  9.67 us
    mul x6, other arithmetic, on_device(): scaled = tuple((summed_grad * scale_factor for summed_grad in shares))  7.77 us
    all_to_all x1, waiting for transfers between devices, on_device(): lax.all_to_all(outgoing, 'graph', split_axis=0, concat_axis=0, tiled=True)  6.64 us
  transfers between devices with their start and end apart: 5, of which 3 were waited for; matrix products, arithmetic and copies ran while one was open for 12% of the time, Pallas kernels for 0%

profile of v1, /device:TPU:0, one launch (start us, length us, event | category | flops | bytes accessed | tf_op | source)
XLA Modules:
  0.0 297.2 jit_solution(1531489678884279180)
XLA Ops:
  7.2 0.8 compare_bitcast_fusion
  8.1 0.7 fusion.59
  8.8 0.7 scatter_custom_fusion.1
  9.5 0.7 all_to_all.14
  10.2 5.2 %all-to-all-start = ((s32[8,4,1]{1,2,0:T(1,128)}), s32[8,4,1]{1,2,0:T(1,128)S(1)}, u32[]{:S(2)}, u32[]{:S(2)}) async-start(s32[8,4,1]{1,2,0:T(1,128)} %bitcast.11), calls=%async_computation | async-start | bytes 8192 | tf_op jit(solution)/shard_map/all_to_all | solution.py:183
  15.4 1.3 iota_compare_fusion
  17.4 1.2 fusion.43
  18.6 1.2 convolution_convert_fusion.1
  20.3 1.2 gather_fusion.1
  21.5 1.2 gather_fusion
  22.7 2.4 scatter_custom_fusion
  25.6 0.9 broadcast_in_dim.80
  26.4 2.1 scatter_fusion
  28.5 4.2 %all-to-all-start.1 = ((bf16[32,32,256]{2,1,0:T(8,128)(2,1)}), bf16[32,32,256]{2,1,0:T(8,128)(2,1)}, u32[]{:S(2)}, u32[]{:S(2)}) async-start(bf16[32,32,256]{2,1,0:T(8,128)(2,1)} %scatter_fusion), calls=%async_computation.1 | async-start | bytes 1048576 | tf_op jit(solution)/shard_map/all_to_all | solution.py:182
  33.0 0.8 bitcast_select_fusion
  35.9 6.6 %all-to-all-done.1 = bf16[32,32,256]{2,1,0:T(8,128)(2,1)} async-done(((bf16[32,32,256]{2,1,0:T(8,128)(2,1)}), bf16[32,32,256]{2,1,0:T(8,128)(2,1)}, u32[]{:S(2)}, u32[]{:S(2)}) %all-to-all-start.1) | async-done | bytes 524320 | tf_op jit(solution)/shard_map/all_to_all | solution.py:182
  42.6 1.6 gather_fusion.3
  44.4 0.8 fusion.72
  46.6 2.0 convert_reduce_fusion
  49.2 1.1 fusion.47
  50.5 1.1 fusion.75
  51.6 1.1 convolution_bitcast_fusion
  52.7 1.1 fusion.71
  53.8 1.2 gather_fusion.5
  55.0 2.6 scatter_custom_fusion.4
  57.6 2.6 scatter_custom_fusion.5
  60.7 1.0 pad_maximum_fusion.1
  61.8 1.3 pad_maximum_fusion
  63.9 1.9 fusion.73
  66.0 0.7 fusion.52
  66.7 134.0 %all-reduce.9.cloned.1.call-done = (f32[512,512]{1,0:T(8,128)}, f32[512,256]{1,0:T(8,128)}, f32[768,512]{1,0:T(8,128)}, f32[512,256]{1,0:T(8,128)}) async-done(((f32[512,512]{1,0:T(8,128)}, f32[512,256]{1,0:T(8,128)}, f32[768,512]{1,0:T(8,128)}, f32[512,256]{1,0:T(8,128)}), (f32[512,512]{1,0:T(8,128)}, f32[512,256]{1,0:T(8,128)}, f32[768,512]{1,0:T(8,128)}, ...) | async-done | bytes 3670032 | tf_op jit(solution)/shard_map/psum | solution.py:223
  200.7 2.2 convolution_add_fusion
  203.0 1.3 scatter_fusion.1
  204.4 0.9 convert_element_type.113
  205.3 3.7 %all-to-all-start.2 = ((bf16[32,32,256]{2,1,0:T(8,128)(2,1)}), bf16[32,32,256]{2,1,0:T(8,128)(2,1)S(1)}, u32[]{:S(2)}, u32[]{:S(2)}) async-start(bf16[32,32,256]{2,1,0:T(8,128)(2,1)} %convert_element_type.113), calls=%async_computation.2 | async-start | bytes 1048576 | tf_op jit(solution)/shard_map/all_to_all | solution.py:213
  209.0 9.7 %all-reduce.2 = (f32[512]{0:T(512)S(1)}, f32[512]{0:T(512)S(1)}) all-reduce(f32[512]{0:T(512)S(1)} %convert_reduce_fusion.1, f32[512]{0:T(512)S(1)} %copy-done.21), channel_id=1, replica_groups=mesh['graph'=8,'rep'=4] {'rep'}, use_global_device_ids=true, to_apply=%region_12.13 | all-reduce | flops 1024 | bytes 8192 | tf_op jit(solution)/shard_map/psum | solution.py:223
  218.7 13.1 %all-reduce = (f32[512]{0:T(512)S(1)}, f32[512]{0:T(512)S(1)}) all-reduce(f32[512]{0:T(512)S(1)} %get-tuple-element.14, f32[512]{0:T(512)S(1)} %get-tuple-element.15), channel_id=1, replica_groups=mesh['graph'=8,'rep'=4] {'graph'}, use_global_device_ids=true, to_apply=%region_13.14 | all-reduce | flops 1024 | bytes 8192 | tf_op jit(solution)/shard_map/psum | solution.py:234
  233.2 2.0 fusion.11
  235.2 1.1 convert_element_type.114
  236.4 1.9 gather_fusion.4
  238.3 2.2 fusion.6
  240.5 1.2 fusion.7
  241.7 0.9 fusion.13
  242.6 41.2 %all-reduce.7.cloned.1.call-done = (f32[512,512]{1,0:T(8,128)}, f32[512,256]{1,0:T(8,128)}, f32[768,512]{1,0:T(8,128)}, f32[512,256]{1,0:T(8,128)}) async-done(((f32[512,512]{1,0:T(8,128)}, f32[512,256]{1,0:T(8,128)}, f32[768,512]{1,0:T(8,128)}, f32[512,256]{1,0:T(8,128)}), (f32[512,512]{1,0:T(8,128)}, f32[512,256]{1,0:T(8,128)}, f32[768,512]{1,0:T(8,128)}, ...) | async-done | bytes 3670032 | tf_op jit(solution)/shard_map/psum | solution.py:234
  283.8 1.7 dynamic-slice_multiply_fusion.1
  285.5 1.6 dynamic-slice_multiply_fusion.3
  287.0 1.6 dynamic-slice_multiply_fusion.2
  288.6 1.8 dynamic-slice_multiply_fusion
  (95 shorter events, 9.5 us)
Async XLA Ops:
  7.2 39.4 %copy-start = (bf16[512,256]{1,0:T(8,128)(2,1)S(1)}, bf16[512,256]{1,0:T(8,128)(2,1)}, u32[]{:S(2)}) copy-start(bf16[512,256]{1,0:T(8,128)(2,1)} %param.24) | copy-start | bytes 786436
  7.2 12.7 %copy-start.1 = (bf16[1,8,32,256]{3,2,1,0:T(8,128)(2,1)S(1)}, bf16[1,8,32,256]{3,2,1,0:T(8,128)(2,1)}, u32[]{:S(2)}) copy-start(bf16[1,8,32,256]{3,2,1,0:T(8,128)(2,1)} %param.13) | copy-start | bytes 393220
  7.2 12.7 %copy-start.5 = (bf16[512,512]{1,0:T(8,128)(2,1)S(1)}, bf16[512,512]{1,0:T(8,128)(2,1)}, u32[]{:S(2)}) copy-start(bf16[512,512]{1,0:T(8,128)(2,1)} %param.19) | copy-start | bytes 1572868
  7.2 12.7 %copy-start.22 = (s32[1,256]{1,0:T(1,128)S(1)}, s32[1,256]{1,0:T(1,128)}, u32[]{:S(2)}) copy-start(s32[1,256]{1,0:T(1,128)} %param.18) | copy-start | bytes 3076
  7.2 12.7 %copy-start.23 = (s32[1,256]{1,0:T(1,128)S(1)}, s32[1,256]{1,0:T(1,128)}, u32[]{:S(2)}) copy-start(s32[1,256]{1,0:T(1,128)} %param.17) | copy-start | bytes 3076
  7.2 12.7 %copy-start.17 = (f32[512]{0:T(512)S(1)}, f32[512]{0:T(512)}, u32[]{:S(2)}) copy-start(f32[512]{0:T(512)} %param.20) | copy-start | bytes 6148
  10.2 18.3 %all-to-all-start = ((s32[8,4,1]{1,2,0:T(1,128)}), s32[8,4,1]{1,2,0:T(1,128)S(1)}, u32[]{:S(2)}, u32[]{:S(2)}) async-start(s32[8,4,1]{1,2,0:T(1,128)} %bitcast.11), calls=%async_computation | async-start | bytes 8192 | tf_op jit(solution)/shard_map/all_to_all | solution.py:183
  17.4 2.9 copy-start.19
  21.5 3.6 %copy-start.7 = (bf16[512,256]{1,0:T(8,128)(2,1)S(1)}, bf16[512,256]{1,0:T(8,128)(2,1)}, u32[]{:S(2)}) copy-start(bf16[512,256]{1,0:T(8,128)(2,1)} %param.21) | copy-start | bytes 786436
  22.7 2.6 copy-start.2
  25.3 7.7 %copy-start.15 = (bf16[1,8,32,256]{3,2,1,0:T(8,128)(2,1)S(1)}, bf16[1,8,32,256]{3,2,1,0:T(8,128)(2,1)}, u32[]{:S(2)}) copy-start(bf16[1,8,32,256]{3,2,1,0:T(8,128)(2,1)} %param.14) | copy-start | bytes 393220
  25.6 7.2 %copy-start.24 = (pred[8,32]{1,0:T(8,128)(4,1)S(1)}, pred[8,32]{1,0:T(8,128)(4,1)}, u32[]{:S(2)}) copy-start(pred[8,32]{1,0:T(8,128)(4,1)} %iota_compare_fusion) | copy-start | bytes 772
  28.5 14.0 %all-to-all-start.1 = ((bf16[32,32,256]{2,1,0:T(8,128)(2,1)}), bf16[32,32,256]{2,1,0:T(8,128)(2,1)}, u32[]{:S(2)}, u32[]{:S(2)}) async-start(bf16[32,32,256]{2,1,0:T(8,128)(2,1)} %scatter_fusion), calls=%async_computation.1 | async-start | bytes 1048576 | tf_op jit(solution)/shard_map/all_to_all | solution.py:182
  32.7 167.9 %all-reduce.9.cloned.1.call-start = ((), (), s32[]{:S(2)}) async-start(), calls=%async_computation.4 | async-start | bytes 7340032 | tf_op jit(solution)/shard_map/psum | solution.py:223
  35.7 10.7 %copy-start.18 = (f32[512]{0:T(512)S(1)}, f32[512]{0:T(512)}, u32[]{:S(2)}) copy-start(f32[512]{0:T(512)} %param.23) | copy-start | bytes 6148
  45.7 0.7 copy-start.12
  46.6 6.1 %copy-start.11 = (f32[256,512]{1,0:T(8,128)}, f32[256,512]{1,0:T(8,128)S(1)}, u32[]{:S(2)}) copy-start(f32[256,512]{1,0:T(8,128)S(1)} %fusion.2) | copy-start | bytes 1572868
  46.6 2.3 copy-start.8
  48.6 1.6 copy-start.13
  50.3 2.4 copy-start.9
  60.4 1.3 copy-start.3
  60.4 1.3 copy-start.4
  63.1 0.7 copy-start.20
  63.1 220.7 %all-reduce.7.cloned.1.call-start = ((), (), s32[]{:S(2)}) async-start(), calls=%async_computation.3 | async-start | bytes 7340032 | tf_op jit(solution)/shard_map/psum | solution.py:234
  66.0 134.7 %copy-start.14 = (f32[8,32,64]{2,1,0:T(8,128)}, f32[8,32,64]{2,1,0:T(8,128)S(1)}, u32[]{:S(2)}) copy-start(f32[8,32,64]{2,1,0:T(8,128)S(1)} %fusion.74) | copy-start | bytes 196612
  204.4 4.6 %copy-start.21 = (f32[512]{0:T(512)S(1)}, f32[512]{0:T(512)}, u32[]{:S(2)}) copy-start(f32[512]{0:T(512)} %get-tuple-element.24) | copy-start | bytes 6148
  204.4 28.6 %copy-start.6 = (bf16[512,512]{1,0:T(8,128)(2,1)S(1)}, bf16[512,512]{1,0:T(8,128)(2,1)}, u32[]{:S(2)}) copy-start(bf16[512,512]{1,0:T(8,128)(2,1)} %param.19) | copy-start | bytes 1572868
  205.3 30.0 %all-to-all-start.2 = ((bf16[32,32,256]{2,1,0:T(8,128)(2,1)}), bf16[32,32,256]{2,1,0:T(8,128)(2,1)S(1)}, u32[]{:S(2)}, u32[]{:S(2)}) async-start(bf16[32,32,256]{2,1,0:T(8,128)(2,1)} %convert_element_type.113), calls=%async_computation.2 | async-start | bytes 1048576 | tf_op jit(solution)/shard_map/all_to_all | solution.py:213
  235.2 3.1 %copy-start.16 = (bf16[256,256]{1,0:T(8,128)(2,1)S(1)}, bf16[256,256]{1,0:T(8,128)(2,1)}, u32[]{:S(2)}) copy-start(bf16[256,256]{1,0:T(8,128)(2,1)} %get-tuple-element.23) | copy-start | bytes 393220
  235.2 5.3 %copy-start.10 = (bf16[256,256]{1,0:T(8,128)(2,1)S(1)}, bf16[256,256]{1,0:T(8,128)(2,1)}, u32[]{:S(2)}) copy-start(bf16[256,256]{1,0:T(8,128)(2,1)} %bitcast_select_fusion) | copy-start | bytes 393220
Sparse Core Ops, SparseCore 0:
  63.2 137.3 all-reduce.8
  204.3 79.4 all-reduce.6
